TPU v7x, 256 devices: a whole 4x4x8 slice. The times are simulated.
256 devices in a mesh: section: 8 (over z_hi, x), dp: 32 (over z_lo, y, core).
Axes of the slice: x: 4, y: 4, z: 8 (z_hi: 2, z_lo: 4; z = z_hi * 4 + z_lo), core: 2. Of those that a mesh axis runs over, the one named last changes fastest.
Arguments:
- features: bfloat16 [1, 8, 4096, 4096], P(None, 'section', 'dp'), parts along dimension 2, may hold values from -6 to 6
- in_proj: bfloat16 [8, 4096, 512], P('section'), may hold values from -0.09375 to 0.09375
- mix_proj: bfloat16 [8, 2, 256, 256], P('section'), may hold values from -0.375 to 0.375
- out_proj: bfloat16 [8, 512, 4096], P('section'), may hold values from -0.375 to 0.375
- gate_proj: bfloat16 [8, 2, 4096], P('section'), may hold values from -0.09375 to 0.09375
- cross_bias: float32 [8, 4096], P('section'), may hold values from -3 to 3
Outputs:
- crossed: bfloat16 [1, 8, 4096, 4096], P(None, 'section', 'dp'), parts along dimension 2
There are 32 independent parts, one for each index of `dp`. A program takes and returns all parts, laid end to end along the dimension named above; an argument that names none is the same for every part. Nothing has to cross between parts.
All inputs are finite; a program needn't handle non-finite values.
Results may differ from a plain program's by a relative error of at most 0.015.
Values may be sent and summed in bfloat16 or wider, within the bound.
A program may use at most 64 MiB of HBM per device.

v0:
```python
import jax
import jax.numpy as jnp
from jax import lax
from jax.sharding import PartitionSpec as P


def from_behind(block, axis, distance):
    devices = range(lax.axis_size(axis))
    route = [(i - distance, i) for i in devices if i - distance in devices]
    return lax.ppermute(block, axis, route)


def cross_layer(current, anchor, v_mat, c_mat, u_mat, gate_mat, shift_row):
    row_count = current.shape[0]
    expert_count = c_mat.shape[0]
    rank_size = c_mat.shape[1]
    projected = jnp.dot(current, v_mat, preferred_element_type=jnp.float32)
    inner_first = (
        jnp.tanh(projected).astype(jnp.bfloat16).reshape(row_count, expert_count, rank_size)
    )
    inner_second = jnp.einsum(
        "rek,ekj->rej", inner_first, c_mat, preferred_element_type=jnp.float32
    )
    logits = lax.dot_general(
        current, gate_mat, (((1,), (1,)), ((), ())), preferred_element_type=jnp.float32
    )
    gate_values = 1.0 / jnp.sum(jnp.exp(logits[:, None, :] - logits[:, :, None]), axis=2)
    blended = (gate_values[:, :, None] * jnp.tanh(inner_second)).astype(jnp.bfloat16)
    blended = blended.reshape(row_count, expert_count * rank_size)
    crossed = jnp.dot(blended, u_mat, preferred_element_type=jnp.float32)
    updated = current.astype(jnp.float32) + anchor.astype(jnp.float32) * (crossed + shift_row)
    return updated.astype(jnp.bfloat16)


def per_device(features, in_proj, mix_proj, out_proj, gate_proj, cross_bias):
    section_count = lax.axis_size("section")
    position = lax.axis_index("section")
    pieces = 2
    local_micro = features.shape[0]
    row_count = features.shape[2]
    feature_count = features.shape[3]
    piece_rows = row_count // pieces
    everyone = lax.all_gather(features, "section", axis=1, tiled=True)
    all_units = everyone.reshape(local_micro * section_count * pieces, piece_rows, feature_count)
    unit_count = all_units.shape[0]
    step_count = unit_count + section_count - 1
    v_mat = in_proj[0]
    c_mat = mix_proj[0]
    u_mat = out_proj[0]
    gate_mat = gate_proj[0]
    shift_row = cross_bias[0]

    def apply_layer(current, anchor):
        return cross_layer(current, anchor, v_mat, c_mat, u_mat, gate_mat, shift_row)

    def keep_input(current, anchor):
        return current

    def advance(carried, moment):
        incoming, outgoing, collected = carried
        unit_here = moment - position
        active = (unit_here >= 0) & (unit_here < unit_count)
        anchor = lax.dynamic_index_in_dim(
            all_units, jnp.clip(unit_here, 0, unit_count - 1), 0, keepdims=False
        )
        current = jnp.where(position == 0, anchor, incoming)
        result = lax.cond(active, apply_layer, keep_input, current, anchor)
        outgoing = jnp.where(position == section_count - 1, result, outgoing)
        held_unit = moment + position - 2 * section_count + 2
        arrived = (
            (held_unit >= 0)
            & (held_unit < unit_count)
            & (held_unit // pieces % section_count == position)
        )
        held_safe = jnp.clip(held_unit, 0, unit_count - 1)
        slot_index = held_safe // pieces // section_count * pieces + held_safe % pieces
        previous = lax.dynamic_index_in_dim(collected, slot_index, 0, keepdims=False)
        collected = lax.dynamic_update_index_in_dim(
            collected, jnp.where(arrived, outgoing, previous), slot_index, 0
        )
        return (result, outgoing, collected)

    def forward_step(carried, moment):
        result, outgoing, collected = advance(carried, moment)
        incoming = from_behind(result, "section", 1)
        return ((incoming, outgoing, collected), None)

    def cycle_step(carried, moment):
        moved, _ = forward_step(carried, moment)
        incoming, outgoing, collected = moved
        outgoing = from_behind(outgoing, "section", -1)
        return ((incoming, outgoing, collected), None)

    blank = jnp.zeros((piece_rows, feature_count), jnp.bfloat16)
    holding = jnp.zeros((local_micro * pieces, piece_rows, feature_count), jnp.bfloat16)
    carried, _ = lax.scan(
        forward_step, (blank, blank, holding), jnp.arange(0, section_count - 1, dtype=jnp.int32)
    )
    carried, _ = lax.scan(
        cycle_step, carried, jnp.arange(section_count - 1, step_count - 1, dtype=jnp.int32)
    )
    _, _, collected = advance(carried, jnp.int32(step_count - 1))
    return collected.reshape(local_micro, 1, row_count, feature_count)


def solution(mesh):
    placed = (
        P(None, "section", "dp", None),
        P("section", None, None),
        P("section", None, None, None),
        P("section", None, None),
        P("section", None, None),
        P("section", None),
    )
    return jax.shard_map(
        per_device,
        mesh=mesh,
        in_specs=placed,
        out_specs=P(None, "section", "dp", None),
        check_vma=False,
    )
```

profile of v0, /device:TPU:160, one launch (start us, length us, event | category | flops | bytes accessed | tf_op | source)
XLA Modules:
  0.0 966.1 jit_solution(16218471225976274042)
XLA Ops:
  7.3 171.0 %all-gather.2.cloned.1.call-done = bf16[1,8,128,4096]{3,2,0,1:T(8,128)(2,1)} async-done(((bf16[1,1,128,4096]{3,2,0,1:T(8,128)(2,1)}), bf16[1,8,128,4096]{3,2,0,1:T(8,128)(2,1)}) %all-gather.2.cloned.1.call-update) | async-done | bytes 8388624 | tf_op jit(solution)/shard_map/all_gather | solution.py:43
  179.5 250.9 %while.40 = (s32[]{:T(128)}, bf16[64,4096]{1,0:T(8,128)(2,1)S(1)}, bf16[64,4096]{1,0:T(8,128)(2,1)S(1)}, bf16[2,64,4096]{2,1,0:T(8,128)(2,1)}, s32[7]{0:T(128)S(...) while((s32[]{:T(128)}, bf16[64,4096]{1,0:T(8,128)(2,1)S(1)}, ...), condition=%wide.region_4.5_spmd.clone, body=%wide.region_0.4_spmd.clone.sunk | while | flops 557416960 | bytes 37524112 | solution.py:96
  187.0 31.3 %collective-permute-done.2 = bf16[64,4096]{1,0:T(8,128)(2,1)S(1)} collective-permute-done((bf16[64,4096]{1,0:T(8,128)(2,1)S(1)}, bf16[64,4096]{1,0:T(8,128)(2,1)S(1)}, u32[]{:S(2)}, u32[]{:S(2)}) %collective-permute-start.2) | collective-permute-done | bytes 524320 | tf_op jit(solution)/shard_map/while/body/eval_jaxpr/ppermute | solution.py:10
  225.5 36.1 %collective-permute-done.2 = bf16[64,4096]{1,0:T(8,128)(2,1)S(1)} collective-permute-done((bf16[64,4096]{1,0:T(8,128)(2,1)S(1)}, bf16[64,4096]{1,0:T(8,128)(2,1)S(1)}, u32[]{:S(2)}, u32[]{:S(2)}) %collective-permute-start.2) | collective-permute-done | bytes 524320 | tf_op jit(solution)/shard_map/while/body/eval_jaxpr/ppermute | solution.py:10
  268.8 25.8 %collective-permute-done.2 = bf16[64,4096]{1,0:T(8,128)(2,1)S(1)} collective-permute-done((bf16[64,4096]{1,0:T(8,128)(2,1)S(1)}, bf16[64,4096]{1,0:T(8,128)(2,1)S(1)}, u32[]{:S(2)}, u32[]{:S(2)}) %collective-permute-start.2) | collective-permute-done | bytes 524320 | tf_op jit(solution)/shard_map/while/body/eval_jaxpr/ppermute | solution.py:10
  301.8 23.0 %collective-permute-done.2 = bf16[64,4096]{1,0:T(8,128)(2,1)S(1)} collective-permute-done((bf16[64,4096]{1,0:T(8,128)(2,1)S(1)}, bf16[64,4096]{1,0:T(8,128)(2,1)S(1)}, u32[]{:S(2)}, u32[]{:S(2)}) %collective-permute-start.2) | collective-permute-done | bytes 524320 | tf_op jit(solution)/shard_map/while/body/eval_jaxpr/ppermute | solution.py:10
  327.2 4.8 conditional.8
  336.9 27.7 %collective-permute-done.2 = bf16[64,4096]{1,0:T(8,128)(2,1)S(1)} collective-permute-done((bf16[64,4096]{1,0:T(8,128)(2,1)S(1)}, bf16[64,4096]{1,0:T(8,128)(2,1)S(1)}, u32[]{:S(2)}, u32[]{:S(2)}) %collective-permute-start.2) | collective-permute-done | bytes 524320 | tf_op jit(solution)/shard_map/while/body/eval_jaxpr/ppermute | solution.py:10
  367.0 4.8 conditional.8
  376.6 21.3 %collective-permute-done.2 = bf16[64,4096]{1,0:T(8,128)(2,1)S(1)} collective-permute-done((bf16[64,4096]{1,0:T(8,128)(2,1)S(1)}, bf16[64,4096]{1,0:T(8,128)(2,1)S(1)}, u32[]{:S(2)}, u32[]{:S(2)}) %collective-permute-start.2) | collective-permute-done | bytes 524320 | tf_op jit(solution)/shard_map/while/body/eval_jaxpr/ppermute | solution.py:10
  400.3 4.8 conditional.8
  409.9 20.4 %collective-permute-done.2 = bf16[64,4096]{1,0:T(8,128)(2,1)S(1)} collective-permute-done((bf16[64,4096]{1,0:T(8,128)(2,1)S(1)}, bf16[64,4096]{1,0:T(8,128)(2,1)S(1)}, u32[]{:S(2)}, u32[]{:S(2)}) %collective-permute-start.2) | collective-permute-done | bytes 524320 | tf_op jit(solution)/shard_map/while/body/eval_jaxpr/ppermute | solution.py:10
  430.3 525.7 %while.39 = (s32[]{:T(128)}, bf16[64,4096]{1,0:T(8,128)(2,1)S(1)}, bf16[64,4096]{1,0:T(8,128)(2,1)S(1)}, bf16[2,64,4096]{2,1,0:T(8,128)(2,1)}, s32[15]{0:T(128)S...) while((s32[]{:T(128)}, bf16[64,4096]{1,0:T(8,128)(2,1)S(1)}, ...), condition=%wide.region_9.10_spmd, body=%wide.region_5.9_spmd.sunk | while | flops 557154816 | bytes 39621292 | solution.py:99
  434.6 4.8 conditional.7
  442.3 3.9 collective-permute-start
  446.2 12.7 %collective-permute-done.1 = bf16[64,4096]{1,0:T(8,128)(2,1)S(1)} collective-permute-done((bf16[64,4096]{1,0:T(8,128)(2,1)S(1)}, bf16[64,4096]{1,0:T(8,128)(2,1)S(1)}, u32[]{:S(2)}, u32[]{:S(2)}) %collective-permute-start.1) | collective-permute-done | bytes 524320 | tf_op jit(solution)/shard_map/while/body/eval_jaxpr/ppermute | solution.py:10
  459.0 10.1 %collective-permute-done = bf16[64,4096]{1,0:T(8,128)(2,1)S(1)} collective-permute-done((bf16[64,4096]{1,0:T(8,128)(2,1)S(1)}, bf16[64,4096]{1,0:T(8,128)(2,1)S(1)}, u32[]{:S(2)}, u32[]{:S(2)}) %collective-permute-start) | collective-permute-done | bytes 524320 | tf_op jit(solution)/shard_map/while/body/eval_jaxpr/ppermute | solution.py:10
  473.3 4.8 conditional.7
  481.1 3.9 collective-permute-start
  485.0 13.6 %collective-permute-done.1 = bf16[64,4096]{1,0:T(8,128)(2,1)S(1)} collective-permute-done((bf16[64,4096]{1,0:T(8,128)(2,1)S(1)}, bf16[64,4096]{1,0:T(8,128)(2,1)S(1)}, u32[]{:S(2)}, u32[]{:S(2)}) %collective-permute-start.1) | collective-permute-done | bytes 524320 | tf_op jit(solution)/shard_map/while/body/eval_jaxpr/ppermute | solution.py:10
  498.6 10.1 %collective-permute-done = bf16[64,4096]{1,0:T(8,128)(2,1)S(1)} collective-permute-done((bf16[64,4096]{1,0:T(8,128)(2,1)S(1)}, bf16[64,4096]{1,0:T(8,128)(2,1)S(1)}, u32[]{:S(2)}, u32[]{:S(2)}) %collective-permute-start) | collective-permute-done | bytes 524320 | tf_op jit(solution)/shard_map/while/body/eval_jaxpr/ppermute | solution.py:10
  512.9 4.8 conditional.7
  524.6 17.9 %collective-permute-done.1 = bf16[64,4096]{1,0:T(8,128)(2,1)S(1)} collective-permute-done((bf16[64,4096]{1,0:T(8,128)(2,1)S(1)}, bf16[64,4096]{1,0:T(8,128)(2,1)S(1)}, u32[]{:S(2)}, u32[]{:S(2)}) %collective-permute-start.1) | collective-permute-done | bytes 524320 | tf_op jit(solution)/shard_map/while/body/eval_jaxpr/ppermute | solution.py:10
  542.5 10.4 %collective-permute-done = bf16[64,4096]{1,0:T(8,128)(2,1)S(1)} collective-permute-done((bf16[64,4096]{1,0:T(8,128)(2,1)S(1)}, bf16[64,4096]{1,0:T(8,128)(2,1)S(1)}, u32[]{:S(2)}, u32[]{:S(2)}) %collective-permute-start) | collective-permute-done | bytes 524320 | tf_op jit(solution)/shard_map/while/body/eval_jaxpr/ppermute | solution.py:10
  557.1 4.8 conditional.7
  564.9 3.9 collective-permute-start
  568.8 9.9 %collective-permute-done.1 = bf16[64,4096]{1,0:T(8,128)(2,1)S(1)} collective-permute-done((bf16[64,4096]{1,0:T(8,128)(2,1)S(1)}, bf16[64,4096]{1,0:T(8,128)(2,1)S(1)}, u32[]{:S(2)}, u32[]{:S(2)}) %collective-permute-start.1) | collective-permute-done | bytes 524320 | tf_op jit(solution)/shard_map/while/body/eval_jaxpr/ppermute | solution.py:10
  578.7 8.3 collective-permute-done
  591.2 4.8 conditional.7
  599.0 3.9 collective-permute-start
  602.9 12.8 %collective-permute-done.1 = bf16[64,4096]{1,0:T(8,128)(2,1)S(1)} collective-permute-done((bf16[64,4096]{1,0:T(8,128)(2,1)S(1)}, bf16[64,4096]{1,0:T(8,128)(2,1)S(1)}, u32[]{:S(2)}, u32[]{:S(2)}) %collective-permute-start.1) | collective-permute-done | bytes 524320 | tf_op jit(solution)/shard_map/while/body/eval_jaxpr/ppermute | solution.py:10
  615.7 10.1 %collective-permute-done = bf16[64,4096]{1,0:T(8,128)(2,1)S(1)} collective-permute-done((bf16[64,4096]{1,0:T(8,128)(2,1)S(1)}, bf16[64,4096]{1,0:T(8,128)(2,1)S(1)}, u32[]{:S(2)}, u32[]{:S(2)}) %collective-permute-start) | collective-permute-done | bytes 524320 | tf_op jit(solution)/shard_map/while/body/eval_jaxpr/ppermute | solution.py:10
  630.1 4.8 conditional.7
  641.8 17.2 %collective-permute-done.1 = bf16[64,4096]{1,0:T(8,128)(2,1)S(1)} collective-permute-done((bf16[64,4096]{1,0:T(8,128)(2,1)S(1)}, bf16[64,4096]{1,0:T(8,128)(2,1)S(1)}, u32[]{:S(2)}, u32[]{:S(2)}) %collective-permute-start.1) | collective-permute-done | bytes 524320 | tf_op jit(solution)/shard_map/while/body/eval_jaxpr/ppermute | solution.py:10
  658.9 10.4 %collective-permute-done = bf16[64,4096]{1,0:T(8,128)(2,1)S(1)} collective-permute-done((bf16[64,4096]{1,0:T(8,128)(2,1)S(1)}, bf16[64,4096]{1,0:T(8,128)(2,1)S(1)}, u32[]{:S(2)}, u32[]{:S(2)}) %collective-permute-start) | collective-permute-done | bytes 524320 | tf_op jit(solution)/shard_map/while/body/eval_jaxpr/ppermute | solution.py:10
  673.6 4.8 conditional.7
  685.2 9.9 %collective-permute-done.1 = bf16[64,4096]{1,0:T(8,128)(2,1)S(1)} collective-permute-done((bf16[64,4096]{1,0:T(8,128)(2,1)S(1)}, bf16[64,4096]{1,0:T(8,128)(2,1)S(1)}, u32[]{:S(2)}, u32[]{:S(2)}) %collective-permute-start.1) | collective-permute-done | bytes 524320 | tf_op jit(solution)/shard_map/while/body/eval_jaxpr/ppermute | solution.py:10
  695.1 7.9 collective-permute-done
  707.3 4.8 conditional.7
  715.0 3.9 collective-permute-start
  719.0 18.1 %collective-permute-done.1 = bf16[64,4096]{1,0:T(8,128)(2,1)S(1)} collective-permute-done((bf16[64,4096]{1,0:T(8,128)(2,1)S(1)}, bf16[64,4096]{1,0:T(8,128)(2,1)S(1)}, u32[]{:S(2)}, u32[]{:S(2)}) %collective-permute-start.1) | collective-permute-done | bytes 524320 | tf_op jit(solution)/shard_map/while/body/eval_jaxpr/ppermute | solution.py:10
  737.0 10.1 %collective-permute-done = bf16[64,4096]{1,0:T(8,128)(2,1)S(1)} collective-permute-done((bf16[64,4096]{1,0:T(8,128)(2,1)S(1)}, bf16[64,4096]{1,0:T(8,128)(2,1)S(1)}, u32[]{:S(2)}, u32[]{:S(2)}) %collective-permute-start) | collective-permute-done | bytes 524320 | tf_op jit(solution)/shard_map/while/body/eval_jaxpr/ppermute | solution.py:10
  751.4 4.8 conditional.7
  759.1 3.9 collective-permute-start
  763.1 7.4 collective-permute-done.1
  770.5 10.4 %collective-permute-done = bf16[64,4096]{1,0:T(8,128)(2,1)S(1)} collective-permute-done((bf16[64,4096]{1,0:T(8,128)(2,1)S(1)}, bf16[64,4096]{1,0:T(8,128)(2,1)S(1)}, u32[]{:S(2)}, u32[]{:S(2)}) %collective-permute-start) | collective-permute-done | bytes 524320 | tf_op jit(solution)/shard_map/while/body/eval_jaxpr/ppermute | solution.py:10
  785.1 4.8 conditional.7
  796.8 9.0 collective-permute-done.1
  805.8 7.9 collective-permute-done
  817.9 4.8 conditional.7
  829.6 8.2 collective-permute-done.1
  837.8 7.9 collective-permute-done
  850.0 4.8 conditional.7
  861.6 7.3 collective-permute-done.1
  868.9 7.9 collective-permute-done
  881.1 4.8 conditional.7
  888.9 3.9 collective-permute-start
  892.8 6.4 collective-permute-done.1
  899.2 7.9 collective-permute-done
  918.3 5.6 collective-permute-done.1
  923.9 7.9 collective-permute-done
  939.0 3.9 collective-permute-start
  942.9 5.2 collective-permute-done.1
  948.1 7.9 collective-permute-done
  (374 shorter events, 235.1 us)
Async XLA Ops:
  6.5 171.8 %all-gather.2.cloned.1.call-start = ((), (), s32[]{:S(2)}) async-start(), calls=%async_computation | async-start | bytes 9437184 | tf_op jit(solution)/shard_map/all_gather | solution.py:43
  181.9 36.4 %collective-permute-start.2 = (bf16[64,4096]{1,0:T(8,128)(2,1)S(1)}, bf16[64,4096]{1,0:T(8,128)(2,1)S(1)}, u32[]{:S(2)}, u32[]{:S(2)}) collective-permute-start(bf16[64,4096]{1,0:T(8,128)(2,1)S(1)} %get-tuple-element.1181), channel_id=1, source_target_pairs={{0,32},{32,64},{64,96},{96,128},{128,160},{160,192},{192,224},{1,3... | collective-permute-start | bytes 1572872 | tf_op jit(solution)/shard_map/while/body/eval_jaxpr/ppermute | solution.py:10
  220.7 40.9 %collective-permute-start.2 = (bf16[64,4096]{1,0:T(8,128)(2,1)S(1)}, bf16[64,4096]{1,0:T(8,128)(2,1)S(1)}, u32[]{:S(2)}, u32[]{:S(2)}) collective-permute-start(bf16[64,4096]{1,0:T(8,128)(2,1)S(1)} %get-tuple-element.1181), channel_id=1, source_target_pairs={{0,32},{32,64},{64,96},{96,128},{128,160},{160,192},{192,224},{1,3... | collective-permute-start | bytes 1572872 | tf_op jit(solution)/shard_map/while/body/eval_jaxpr/ppermute | solution.py:10
  264.0 30.6 %collective-permute-start.2 = (bf16[64,4096]{1,0:T(8,128)(2,1)S(1)}, bf16[64,4096]{1,0:T(8,128)(2,1)S(1)}, u32[]{:S(2)}, u32[]{:S(2)}) collective-permute-start(bf16[64,4096]{1,0:T(8,128)(2,1)S(1)} %get-tuple-element.1181), channel_id=1, source_target_pairs={{0,32},{32,64},{64,96},{96,128},{128,160},{160,192},{192,224},{1,3... | collective-permute-start | bytes 1572872 | tf_op jit(solution)/shard_map/while/body/eval_jaxpr/ppermute | solution.py:10
  297.0 27.8 %collective-permute-start.2 = (bf16[64,4096]{1,0:T(8,128)(2,1)S(1)}, bf16[64,4096]{1,0:T(8,128)(2,1)S(1)}, u32[]{:S(2)}, u32[]{:S(2)}) collective-permute-start(bf16[64,4096]{1,0:T(8,128)(2,1)S(1)} %get-tuple-element.1181), channel_id=1, source_target_pairs={{0,32},{32,64},{64,96},{96,128},{128,160},{160,192},{192,224},{1,3... | collective-permute-start | bytes 1572872 | tf_op jit(solution)/shard_map/while/body/eval_jaxpr/ppermute | solution.py:10
  327.3 3.7 copy-start
  327.3 3.7 copy-start.6
  332.0 32.6 %collective-permute-start.2 = (bf16[64,4096]{1,0:T(8,128)(2,1)S(1)}, bf16[64,4096]{1,0:T(8,128)(2,1)S(1)}, u32[]{:S(2)}, u32[]{:S(2)}) collective-permute-start(bf16[64,4096]{1,0:T(8,128)(2,1)S(1)} %get-tuple-element.1181), channel_id=1, source_target_pairs={{0,32},{32,64},{64,96},{96,128},{128,160},{160,192},{192,224},{1,3... | collective-permute-start | bytes 1572872 | tf_op jit(solution)/shard_map/while/body/eval_jaxpr/ppermute | solution.py:10
  367.0 3.7 copy-start
  367.0 3.7 copy-start.6
  371.8 26.1 %collective-permute-start.2 = (bf16[64,4096]{1,0:T(8,128)(2,1)S(1)}, bf16[64,4096]{1,0:T(8,128)(2,1)S(1)}, u32[]{:S(2)}, u32[]{:S(2)}) collective-permute-start(bf16[64,4096]{1,0:T(8,128)(2,1)S(1)} %get-tuple-element.1181), channel_id=1, source_target_pairs={{0,32},{32,64},{64,96},{96,128},{128,160},{160,192},{192,224},{1,3... | collective-permute-start | bytes 1572872 | tf_op jit(solution)/shard_map/while/body/eval_jaxpr/ppermute | solution.py:10
  400.3 3.7 copy-start
  400.3 3.7 copy-start.6
  405.1 25.3 %collective-permute-start.2 = (bf16[64,4096]{1,0:T(8,128)(2,1)S(1)}, bf16[64,4096]{1,0:T(8,128)(2,1)S(1)}, u32[]{:S(2)}, u32[]{:S(2)}) collective-permute-start(bf16[64,4096]{1,0:T(8,128)(2,1)S(1)} %get-tuple-element.1181), channel_id=1, source_target_pairs={{0,32},{32,64},{64,96},{96,128},{128,160},{160,192},{192,224},{1,3... | collective-permute-start | bytes 1572872 | tf_op jit(solution)/shard_map/while/body/eval_jaxpr/ppermute | solution.py:10
  434.6 3.7 copy-start.1
  434.6 3.7 copy-start.7
  440.4 18.6 %collective-permute-start.1 = (bf16[64,4096]{1,0:T(8,128)(2,1)S(1)}, bf16[64,4096]{1,0:T(8,128)(2,1)S(1)}, u32[]{:S(2)}, u32[]{:S(2)}) collective-permute-start(bf16[64,4096]{1,0:T(8,128)(2,1)S(1)} %get-tuple-element.1015), channel_id=1, source_target_pairs={{32,0},{64,32},{96,64},{128,96},{160,128},{192,160},{224,192},{33,... | collective-permute-start | bytes 1572872 | tf_op jit(solution)/shard_map/while/body/eval_jaxpr/ppermute | solution.py:10
  442.3 26.8 %collective-permute-start = (bf16[64,4096]{1,0:T(8,128)(2,1)S(1)}, bf16[64,4096]{1,0:T(8,128)(2,1)S(1)}, u32[]{:S(2)}, u32[]{:S(2)}) collective-permute-start(bf16[64,4096]{1,0:T(8,128)(2,1)S(1)} %get-tuple-element.1180), channel_id=1, source_target_pairs={{0,32},{32,64},{64,96},{96,128},{128,160},{160,192},{192,224},{1,3... | collective-permute-start | bytes 1572872 | tf_op jit(solution)/shard_map/while/body/eval_jaxpr/ppermute | solution.py:10
  473.4 3.7 copy-start.1
  473.4 3.7 copy-start.7
  479.2 19.4 %collective-permute-start.1 = (bf16[64,4096]{1,0:T(8,128)(2,1)S(1)}, bf16[64,4096]{1,0:T(8,128)(2,1)S(1)}, u32[]{:S(2)}, u32[]{:S(2)}) collective-permute-start(bf16[64,4096]{1,0:T(8,128)(2,1)S(1)} %get-tuple-element.1015), channel_id=1, source_target_pairs={{32,0},{64,32},{96,64},{128,96},{160,128},{192,160},{224,192},{33,... | collective-permute-start | bytes 1572872 | tf_op jit(solution)/shard_map/while/body/eval_jaxpr/ppermute | solution.py:10
  481.1 27.6 %collective-permute-start = (bf16[64,4096]{1,0:T(8,128)(2,1)S(1)}, bf16[64,4096]{1,0:T(8,128)(2,1)S(1)}, u32[]{:S(2)}, u32[]{:S(2)}) collective-permute-start(bf16[64,4096]{1,0:T(8,128)(2,1)S(1)} %get-tuple-element.1180), channel_id=1, source_target_pairs={{0,32},{32,64},{64,96},{96,128},{128,160},{160,192},{192,224},{1,3... | collective-permute-start | bytes 1572872 | tf_op jit(solution)/shard_map/while/body/eval_jaxpr/ppermute | solution.py:10
  518.8 23.8 %collective-permute-start.1 = (bf16[64,4096]{1,0:T(8,128)(2,1)S(1)}, bf16[64,4096]{1,0:T(8,128)(2,1)S(1)}, u32[]{:S(2)}, u32[]{:S(2)}) collective-permute-start(bf16[64,4096]{1,0:T(8,128)(2,1)S(1)} %get-tuple-element.1015), channel_id=1, source_target_pairs={{32,0},{64,32},{96,64},{128,96},{160,128},{192,160},{224,192},{33,... | collective-permute-start | bytes 1572872 | tf_op jit(solution)/shard_map/while/body/eval_jaxpr/ppermute | solution.py:10
  520.7 32.2 %collective-permute-start = (bf16[64,4096]{1,0:T(8,128)(2,1)S(1)}, bf16[64,4096]{1,0:T(8,128)(2,1)S(1)}, u32[]{:S(2)}, u32[]{:S(2)}) collective-permute-start(bf16[64,4096]{1,0:T(8,128)(2,1)S(1)} %get-tuple-element.1180), channel_id=1, source_target_pairs={{0,32},{32,64},{64,96},{96,128},{128,160},{160,192},{192,224},{1,3... | collective-permute-start | bytes 1572872 | tf_op jit(solution)/shard_map/while/body/eval_jaxpr/ppermute | solution.py:10
  557.2 3.7 copy-start.1
  557.2 3.7 copy-start.7
  563.0 15.7 %collective-permute-start.1 = (bf16[64,4096]{1,0:T(8,128)(2,1)S(1)}, bf16[64,4096]{1,0:T(8,128)(2,1)S(1)}, u32[]{:S(2)}, u32[]{:S(2)}) collective-permute-start(bf16[64,4096]{1,0:T(8,128)(2,1)S(1)} %get-tuple-element.1015), channel_id=1, source_target_pairs={{32,0},{64,32},{96,64},{128,96},{160,128},{192,160},{224,192},{33,... | collective-permute-start | bytes 1572872 | tf_op jit(solution)/shard_map/while/body/eval_jaxpr/ppermute | solution.py:10
  564.9 22.1 %collective-permute-start = (bf16[64,4096]{1,0:T(8,128)(2,1)S(1)}, bf16[64,4096]{1,0:T(8,128)(2,1)S(1)}, u32[]{:S(2)}, u32[]{:S(2)}) collective-permute-start(bf16[64,4096]{1,0:T(8,128)(2,1)S(1)} %get-tuple-element.1180), channel_id=1, source_target_pairs={{0,32},{32,64},{64,96},{96,128},{128,160},{160,192},{192,224},{1,3... | collective-permute-start | bytes 1572872 | tf_op jit(solution)/shard_map/while/body/eval_jaxpr/ppermute | solution.py:10
  591.3 3.7 copy-start.1
  597.1 18.7 %collective-permute-start.1 = (bf16[64,4096]{1,0:T(8,128)(2,1)S(1)}, bf16[64,4096]{1,0:T(8,128)(2,1)S(1)}, u32[]{:S(2)}, u32[]{:S(2)}) collective-permute-start(bf16[64,4096]{1,0:T(8,128)(2,1)S(1)} %get-tuple-element.1015), channel_id=1, source_target_pairs={{32,0},{64,32},{96,64},{128,96},{160,128},{192,160},{224,192},{33,... | collective-permute-start | bytes 1572872 | tf_op jit(solution)/shard_map/while/body/eval_jaxpr/ppermute | solution.py:10
  599.0 26.9 %collective-permute-start = (bf16[64,4096]{1,0:T(8,128)(2,1)S(1)}, bf16[64,4096]{1,0:T(8,128)(2,1)S(1)}, u32[]{:S(2)}, u32[]{:S(2)}) collective-permute-start(bf16[64,4096]{1,0:T(8,128)(2,1)S(1)} %get-tuple-element.1180), channel_id=1, source_target_pairs={{0,32},{32,64},{64,96},{96,128},{128,160},{160,192},{192,224},{1,3... | collective-permute-start | bytes 1572872 | tf_op jit(solution)/shard_map/while/body/eval_jaxpr/ppermute | solution.py:10
  630.1 3.7 copy-start.1
  630.1 3.7 copy-start.7
  635.9 23.0 %collective-permute-start.1 = (bf16[64,4096]{1,0:T(8,128)(2,1)S(1)}, bf16[64,4096]{1,0:T(8,128)(2,1)S(1)}, u32[]{:S(2)}, u32[]{:S(2)}) collective-permute-start(bf16[64,4096]{1,0:T(8,128)(2,1)S(1)} %get-tuple-element.1015), channel_id=1, source_target_pairs={{32,0},{64,32},{96,64},{128,96},{160,128},{192,160},{224,192},{33,... | collective-permute-start | bytes 1572872 | tf_op jit(solution)/shard_map/while/body/eval_jaxpr/ppermute | solution.py:10
  637.8 31.5 %collective-permute-start = (bf16[64,4096]{1,0:T(8,128)(2,1)S(1)}, bf16[64,4096]{1,0:T(8,128)(2,1)S(1)}, u32[]{:S(2)}, u32[]{:S(2)}) collective-permute-start(bf16[64,4096]{1,0:T(8,128)(2,1)S(1)} %get-tuple-element.1180), channel_id=1, source_target_pairs={{0,32},{32,64},{64,96},{96,128},{128,160},{160,192},{192,224},{1,3... | collective-permute-start | bytes 1572872 | tf_op jit(solution)/shard_map/while/body/eval_jaxpr/ppermute | solution.py:10
  673.6 3.7 copy-start.1
  679.4 15.7 %collective-permute-start.1 = (bf16[64,4096]{1,0:T(8,128)(2,1)S(1)}, bf16[64,4096]{1,0:T(8,128)(2,1)S(1)}, u32[]{:S(2)}, u32[]{:S(2)}) collective-permute-start(bf16[64,4096]{1,0:T(8,128)(2,1)S(1)} %get-tuple-element.1015), channel_id=1, source_target_pairs={{32,0},{64,32},{96,64},{128,96},{160,128},{192,160},{224,192},{33,... | collective-permute-start | bytes 1572872 | tf_op jit(solution)/shard_map/while/body/eval_jaxpr/ppermute | solution.py:10
  681.3 21.8 %collective-permute-start = (bf16[64,4096]{1,0:T(8,128)(2,1)S(1)}, bf16[64,4096]{1,0:T(8,128)(2,1)S(1)}, u32[]{:S(2)}, u32[]{:S(2)}) collective-permute-start(bf16[64,4096]{1,0:T(8,128)(2,1)S(1)} %get-tuple-element.1180), channel_id=1, source_target_pairs={{0,32},{32,64},{64,96},{96,128},{128,160},{160,192},{192,224},{1,3... | collective-permute-start | bytes 1572872 | tf_op jit(solution)/shard_map/while/body/eval_jaxpr/ppermute | solution.py:10
  707.3 3.7 copy-start.1
  707.3 3.7 copy-start.7
  713.1 23.9 %collective-permute-start.1 = (bf16[64,4096]{1,0:T(8,128)(2,1)S(1)}, bf16[64,4096]{1,0:T(8,128)(2,1)S(1)}, u32[]{:S(2)}, u32[]{:S(2)}) collective-permute-start(bf16[64,4096]{1,0:T(8,128)(2,1)S(1)} %get-tuple-element.1015), channel_id=1, source_target_pairs={{32,0},{64,32},{96,64},{128,96},{160,128},{192,160},{224,192},{33,... | collective-permute-start | bytes 1572872 | tf_op jit(solution)/shard_map/while/body/eval_jaxpr/ppermute | solution.py:10
  715.0 32.1 %collective-permute-start = (bf16[64,4096]{1,0:T(8,128)(2,1)S(1)}, bf16[64,4096]{1,0:T(8,128)(2,1)S(1)}, u32[]{:S(2)}, u32[]{:S(2)}) collective-permute-start(bf16[64,4096]{1,0:T(8,128)(2,1)S(1)} %get-tuple-element.1180), channel_id=1, source_target_pairs={{0,32},{32,64},{64,96},{96,128},{128,160},{160,192},{192,224},{1,3... | collective-permute-start | bytes 1572872 | tf_op jit(solution)/shard_map/while/body/eval_jaxpr/ppermute | solution.py:10
  751.4 3.7 copy-start.1
  751.4 3.7 copy-start.7
  757.2 13.3 %collective-permute-start.1 = (bf16[64,4096]{1,0:T(8,128)(2,1)S(1)}, bf16[64,4096]{1,0:T(8,128)(2,1)S(1)}, u32[]{:S(2)}, u32[]{:S(2)}) collective-permute-start(bf16[64,4096]{1,0:T(8,128)(2,1)S(1)} %get-tuple-element.1015), channel_id=1, source_target_pairs={{32,0},{64,32},{96,64},{128,96},{160,128},{192,160},{224,192},{33,... | collective-permute-start | bytes 1572872 | tf_op jit(solution)/shard_map/while/body/eval_jaxpr/ppermute | solution.py:10
  759.1 21.8 %collective-permute-start = (bf16[64,4096]{1,0:T(8,128)(2,1)S(1)}, bf16[64,4096]{1,0:T(8,128)(2,1)S(1)}, u32[]{:S(2)}, u32[]{:S(2)}) collective-permute-start(bf16[64,4096]{1,0:T(8,128)(2,1)S(1)} %get-tuple-element.1180), channel_id=1, source_target_pairs={{0,32},{32,64},{64,96},{96,128},{128,160},{160,192},{192,224},{1,3... | collective-permute-start | bytes 1572872 | tf_op jit(solution)/shard_map/while/body/eval_jaxpr/ppermute | solution.py:10
  790.9 14.9 %collective-permute-start.1 = (bf16[64,4096]{1,0:T(8,128)(2,1)S(1)}, bf16[64,4096]{1,0:T(8,128)(2,1)S(1)}, u32[]{:S(2)}, u32[]{:S(2)}) collective-permute-start(bf16[64,4096]{1,0:T(8,128)(2,1)S(1)} %get-tuple-element.1015), channel_id=1, source_target_pairs={{32,0},{64,32},{96,64},{128,96},{160,128},{192,160},{224,192},{33,... | collective-permute-start | bytes 1572872 | tf_op jit(solution)/shard_map/while/body/eval_jaxpr/ppermute | solution.py:10
  792.8 20.9 %collective-permute-start = (bf16[64,4096]{1,0:T(8,128)(2,1)S(1)}, bf16[64,4096]{1,0:T(8,128)(2,1)S(1)}, u32[]{:S(2)}, u32[]{:S(2)}) collective-permute-start(bf16[64,4096]{1,0:T(8,128)(2,1)S(1)} %get-tuple-element.1180), channel_id=1, source_target_pairs={{0,32},{32,64},{64,96},{96,128},{128,160},{160,192},{192,224},{1,3... | collective-permute-start | bytes 1572872 | tf_op jit(solution)/shard_map/while/body/eval_jaxpr/ppermute | solution.py:10
  818.0 3.7 copy-start.1
  818.0 3.7 copy-start.7
  823.8 14.0 %collective-permute-start.1 = (bf16[64,4096]{1,0:T(8,128)(2,1)S(1)}, bf16[64,4096]{1,0:T(8,128)(2,1)S(1)}, u32[]{:S(2)}, u32[]{:S(2)}) collective-permute-start(bf16[64,4096]{1,0:T(8,128)(2,1)S(1)} %get-tuple-element.1015), channel_id=1, source_target_pairs={{32,0},{64,32},{96,64},{128,96},{160,128},{192,160},{224,192},{33,... | collective-permute-start | bytes 1572872 | tf_op jit(solution)/shard_map/while/body/eval_jaxpr/ppermute | solution.py:10
  825.7 20.0 %collective-permute-start = (bf16[64,4096]{1,0:T(8,128)(2,1)S(1)}, bf16[64,4096]{1,0:T(8,128)(2,1)S(1)}, u32[]{:S(2)}, u32[]{:S(2)}) collective-permute-start(bf16[64,4096]{1,0:T(8,128)(2,1)S(1)} %get-tuple-element.1180), channel_id=1, source_target_pairs={{0,32},{32,64},{64,96},{96,128},{128,160},{160,192},{192,224},{1,3... | collective-permute-start | bytes 1572872 | tf_op jit(solution)/shard_map/while/body/eval_jaxpr/ppermute | solution.py:10
  850.0 3.7 copy-start.1
  850.0 3.7 copy-start.7
  855.8 13.2 %collective-permute-start.1 = (bf16[64,4096]{1,0:T(8,128)(2,1)S(1)}, bf16[64,4096]{1,0:T(8,128)(2,1)S(1)}, u32[]{:S(2)}, u32[]{:S(2)}) collective-permute-start(bf16[64,4096]{1,0:T(8,128)(2,1)S(1)} %get-tuple-element.1015), channel_id=1, source_target_pairs={{32,0},{64,32},{96,64},{128,96},{160,128},{192,160},{224,192},{33,... | collective-permute-start | bytes 1572872 | tf_op jit(solution)/shard_map/while/body/eval_jaxpr/ppermute | solution.py:10
  857.7 19.2 %collective-permute-start = (bf16[64,4096]{1,0:T(8,128)(2,1)S(1)}, bf16[64,4096]{1,0:T(8,128)(2,1)S(1)}, u32[]{:S(2)}, u32[]{:S(2)}) collective-permute-start(bf16[64,4096]{1,0:T(8,128)(2,1)S(1)} %get-tuple-element.1180), channel_id=1, source_target_pairs={{0,32},{32,64},{64,96},{96,128},{128,160},{160,192},{192,224},{1,3... | collective-permute-start | bytes 1572872 | tf_op jit(solution)/shard_map/while/body/eval_jaxpr/ppermute | solution.py:10
  881.1 3.7 copy-start.1
  881.2 3.7 copy-start.7
  886.9 12.3 %collective-permute-start.1 = (bf16[64,4096]{1,0:T(8,128)(2,1)S(1)}, bf16[64,4096]{1,0:T(8,128)(2,1)S(1)}, u32[]{:S(2)}, u32[]{:S(2)}) collective-permute-start(bf16[64,4096]{1,0:T(8,128)(2,1)S(1)} %get-tuple-element.1015), channel_id=1, source_target_pairs={{32,0},{64,32},{96,64},{128,96},{160,128},{192,160},{224,192},{33,... | collective-permute-start | bytes 1572872 | tf_op jit(solution)/shard_map/while/body/eval_jaxpr/ppermute | solution.py:10
  888.9 18.3 %collective-permute-start = (bf16[64,4096]{1,0:T(8,128)(2,1)S(1)}, bf16[64,4096]{1,0:T(8,128)(2,1)S(1)}, u32[]{:S(2)}, u32[]{:S(2)}) collective-permute-start(bf16[64,4096]{1,0:T(8,128)(2,1)S(1)} %get-tuple-element.1180), channel_id=1, source_target_pairs={{0,32},{32,64},{64,96},{96,128},{128,160},{160,192},{192,224},{1,3... | collective-permute-start | bytes 1572872 | tf_op jit(solution)/shard_map/while/body/eval_jaxpr/ppermute | solution.py:10
  912.4 11.4 %collective-permute-start.1 = (bf16[64,4096]{1,0:T(8,128)(2,1)S(1)}, bf16[64,4096]{1,0:T(8,128)(2,1)S(1)}, u32[]{:S(2)}, u32[]{:S(2)}) collective-permute-start(bf16[64,4096]{1,0:T(8,128)(2,1)S(1)} %get-tuple-element.1015), channel_id=1, source_target_pairs={{32,0},{64,32},{96,64},{128,96},{160,128},{192,160},{224,192},{33,... | collective-permute-start | bytes 1572872 | tf_op jit(solution)/shard_map/while/body/eval_jaxpr/ppermute | solution.py:10
  914.4 17.5 %collective-permute-start = (bf16[64,4096]{1,0:T(8,128)(2,1)S(1)}, bf16[64,4096]{1,0:T(8,128)(2,1)S(1)}, u32[]{:S(2)}, u32[]{:S(2)}) collective-permute-start(bf16[64,4096]{1,0:T(8,128)(2,1)S(1)} %get-tuple-element.1180), channel_id=1, source_target_pairs={{0,32},{32,64},{64,96},{96,128},{128,160},{160,192},{192,224},{1,3... | collective-permute-start | bytes 1572872 | tf_op jit(solution)/shard_map/while/body/eval_jaxpr/ppermute | solution.py:10
  937.1 11.1 %collective-permute-start.1 = (bf16[64,4096]{1,0:T(8,128)(2,1)S(1)}, bf16[64,4096]{1,0:T(8,128)(2,1)S(1)}, u32[]{:S(2)}, u32[]{:S(2)}) collective-permute-start(bf16[64,4096]{1,0:T(8,128)(2,1)S(1)} %get-tuple-element.1015), channel_id=1, source_target_pairs={{32,0},{64,32},{96,64},{128,96},{160,128},{192,160},{224,192},{33,... | collective-permute-start | bytes 1572872 | tf_op jit(solution)/shard_map/while/body/eval_jaxpr/ppermute | solution.py:10
  939.0 17.1 %collective-permute-start = (bf16[64,4096]{1,0:T(8,128)(2,1)S(1)}, bf16[64,4096]{1,0:T(8,128)(2,1)S(1)}, u32[]{:S(2)}, u32[]{:S(2)}) collective-permute-start(bf16[64,4096]{1,0:T(8,128)(2,1)S(1)} %get-tuple-element.1180), channel_id=1, source_target_pairs={{0,32},{32,64},{64,96},{96,128},{128,160},{160,192},{192,224},{1,3... | collective-permute-start | bytes 1572872 | tf_op jit(solution)/shard_map/while/body/eval_jaxpr/ppermute | solution.py:10
  (38 other events, 130.9 us)
Sparse Core Ops, SparseCore 0:
  10.0 168.3 all-gather.1
where the time goes:
time: 970 us; the launch traced here: 966 us
  waiting for transfers between devices  654 us (67%)
  starting transfers between devices  101 us (10%)
  matrix products  73.6 us (8%)
  other arithmetic  50.4 us (5%)
  local copies, waits for them, and re-layouts  40.5 us (4%)
  loops' own time  32.8 us (3%)
  between operations  13.5 us (1%)
    ppermute x37, waiting for transfers between devices, from_behind(): return lax.ppermute(block, axis, route)  482 us
    all_gather x1, waiting for transfers between devices, per_device(): everyone = lax.all_gather(features, 'section', axis=1, tiled=True)  171 us
    ppermute x37, starting transfers between devices, from_behind(): return lax.ppermute(block, axis, route)  101 us
    dot_general x16, matrix products, cross_layer(): projected = jnp.dot(current, v_mat, preferred_element_type=jnp.float32)  51 us
    select_n x23, other arithmetic, advance(): current = jnp.where(position == 0, anchor, incoming)  25.7 us
    dynamic_slice x23, local copies, waits for them, and re-layouts, advance(): lax.dynamic_index_in_dim(collected, slot_index, 0, keepdims=False)  24.9 us
    dynamic_update_slice x23, other arithmetic, advance(): lax.dynamic_update_index_in_dim(collected, jnp.where(arrived, outgoing, p...  24 us
    another operation x1, loops' own time, per_device(): lax.scan(cycle_step, carried, jnp.arange(section_count - 1, step_count -...  21 us
  transfers between devices with their start and end apart: 38, of which 38 were waited for; matrix products, arithmetic and copies ran while one was open for 2% of the time, Pallas kernels for 0%

commit v1 on v0

--- a/solution.py
+++ b/solution.py
@@ -40,7 +40,9 @@
     row_count = features.shape[2]
     feature_count = features.shape[3]
     piece_rows = row_count // pieces
-    everyone = lax.all_gather(features, "section", axis=1, tiled=True)
+    everyone = jnp.concatenate(
+        lax.all_to_all(jnp.stack([features] * lax.axis_size("section")), "section", 0, 0), axis=1
+    )
     all_units = everyone.reshape(local_micro * section_count * pieces, piece_rows, feature_count)
     unit_count = all_units.shape[0]
     step_count = unit_count + section_count - 1

time: 970 us -> 932 us (0.961)
  waiting for transfers between devices: 654 us -> 592 us
  starting transfers between devices: 101 us -> 131 us
  between operations: 13.5 us -> 0.05 us
    all_gather x1 -> x0, waiting for transfers between devices: 171 us -> none  [per_device(): everyone = lax.all_gather(features, 'section', axis=1, tiled=True)]
    all_to_all x0 -> x1, waiting for transfers between devices: none -> 164 us  [per_device(): lax.all_to_all(jnp.stack([features] * lax.axis_size('section')), 'section...]
    ppermute x37, waiting for transfers between devices: 482 us -> 428 us  [from_behind(): return lax.ppermute(block, axis, route)]
    ppermute x37, starting transfers between devices: 101 us -> 121 us  [from_behind(): return lax.ppermute(block, axis, route)]
    all_to_all x0 -> x1, starting transfers between devices: none -> 9.8 us  [per_device(): lax.all_to_all(jnp.stack([features] * lax.axis_size('section')), 'section...]
where the time goes in v1:
time: 932 us; the launch traced here: 923 us
  waiting for transfers between devices  592 us (64%)
  starting transfers between devices  131 us (14%)
  matrix products  73.6 us (8%)
  other arithmetic  50.4 us (5%)
  local copies, waits for them, and re-layouts  44.9 us (5%)
  loops' own time  31.4 us (3%)
    ppermute x37, waiting for transfers between devices, from_behind(): return lax.ppermute(block, axis, route)  428 us
    all_to_all x1, waiting for transfers between devices, per_device(): lax.all_to_all(jnp.stack([features] * lax.axis_size('section')), 'section...  164 us
    ppermute x37, starting transfers between devices, from_behind(): return lax.ppermute(block, axis, route)  121 us
    dot_general x16, matrix products, cross_layer(): projected = jnp.dot(current, v_mat, preferred_element_type=jnp.float32)  51 us
    select_n x23, other arithmetic, advance(): current = jnp.where(position == 0, anchor, incoming)  25.7 us
    dynamic_slice x23, local copies, waits for them, and re-layouts, advance(): lax.dynamic_index_in_dim(collected, slot_index, 0, keepdims=False)  24.9 us
    dynamic_update_slice x23, other arithmetic, advance(): lax.dynamic_update_index_in_dim(collected, jnp.where(arrived, outgoing, p...  24 us
    another operation x1, loops' own time, per_device(): lax.scan(cycle_step, carried, jnp.arange(section_count - 1, step_count -...  20.6 us
  transfers between devices with their start and end apart: 38, of which 38 were waited for; matrix products, arithmetic and copies ran while one was open for 2% of the time, Pallas kernels for 0%

profile of v1, /device:TPU:160, one launch (start us, length us, event | category | flops | bytes accessed | tf_op | source)
XLA Modules:
  0.0 923.4 jit_solution(11807377221036130820)
XLA Ops:
  0.0 5.5 stack.2
  5.5 9.8 %all-to-all-start = ((bf16[8,1,1,128,4096]{4,3,2,1,0:T(8,128)(2,1)}), bf16[8,1,1,128,4096]{4,3,2,1,0:T(8,128)(2,1)}, u32[]{:S(2)}, u32[]{:S(2)}) async-start(bf16[8,1,1,128,4096]{4,3,2,1,0:T(8,128)(2,1)} %stack.2), calls=%async_computation | async-start | bytes 16777216 | tf_op jit(solution)/shard_map/all_to_all | solution.py:44
  15.3 164.3 %all-to-all-done = bf16[8,1,1,128,4096]{4,3,2,1,0:T(8,128)(2,1)} async-done(((bf16[8,1,1,128,4096]{4,3,2,1,0:T(8,128)(2,1)}), bf16[8,1,1,128,4096]{4,3,2,1,0:T(8,128)(2,1)}, u32[]{:S(2)}, u32[]{:S(2)}) %all-to-all-start) | async-done | bytes 8388640 | tf_op jit(solution)/shard_map/all_to_all | solution.py:44
  180.8 247.6 %while.40 = (s32[]{:T(128)}, bf16[64,4096]{1,0:T(8,128)(2,1)S(1)}, bf16[64,4096]{1,0:T(8,128)(2,1)S(1)}, bf16[2,64,4096]{2,1,0:T(8,128)(2,1)}, s32[7]{0:T(128)S(...) while((s32[]{:T(128)}, bf16[64,4096]{1,0:T(8,128)(2,1)S(1)}, ...), condition=%wide.region_4.5_spmd.clone, body=%wide.region_0.4_spmd.clone.sunk | while | flops 557416960 | bytes 36344376 | solution.py:98
  183.2 22.2 %collective-permute-start.2 = (bf16[64,4096]{1,0:T(8,128)(2,1)S(1)}, bf16[64,4096]{1,0:T(8,128)(2,1)S(1)}, u32[]{:S(2)}, u32[]{:S(2)}) collective-permute-start(bf16[64,4096]{1,0:T(8,128)(2,1)S(1)} %get-tuple-element.1181), channel_id=1, source_target_pairs={{0,32},{32,64},{64,96},{96,128},{128,160},{160,192},{192,224},{1,3... | collective-permute-start | bytes 1572872 | tf_op jit(solution)/shard_map/while/body/eval_jaxpr/ppermute | solution.py:10
  208.2 23.6 %collective-permute-done.2 = bf16[64,4096]{1,0:T(8,128)(2,1)S(1)} collective-permute-done((bf16[64,4096]{1,0:T(8,128)(2,1)S(1)}, bf16[64,4096]{1,0:T(8,128)(2,1)S(1)}, u32[]{:S(2)}, u32[]{:S(2)}) %collective-permute-start.2) | collective-permute-done | bytes 524320 | tf_op jit(solution)/shard_map/while/body/eval_jaxpr/ppermute | solution.py:10
  239.0 28.5 %collective-permute-done.2 = bf16[64,4096]{1,0:T(8,128)(2,1)S(1)} collective-permute-done((bf16[64,4096]{1,0:T(8,128)(2,1)S(1)}, bf16[64,4096]{1,0:T(8,128)(2,1)S(1)}, u32[]{:S(2)}, u32[]{:S(2)}) %collective-permute-start.2) | collective-permute-done | bytes 524320 | tf_op jit(solution)/shard_map/while/body/eval_jaxpr/ppermute | solution.py:10
  274.7 23.0 %collective-permute-done.2 = bf16[64,4096]{1,0:T(8,128)(2,1)S(1)} collective-permute-done((bf16[64,4096]{1,0:T(8,128)(2,1)S(1)}, bf16[64,4096]{1,0:T(8,128)(2,1)S(1)}, u32[]{:S(2)}, u32[]{:S(2)}) %collective-permute-start.2) | collective-permute-done | bytes 524320 | tf_op jit(solution)/shard_map/while/body/eval_jaxpr/ppermute | solution.py:10
  304.9 17.1 %collective-permute-done.2 = bf16[64,4096]{1,0:T(8,128)(2,1)S(1)} collective-permute-done((bf16[64,4096]{1,0:T(8,128)(2,1)S(1)}, bf16[64,4096]{1,0:T(8,128)(2,1)S(1)}, u32[]{:S(2)}, u32[]{:S(2)}) %collective-permute-start.2) | collective-permute-done | bytes 524320 | tf_op jit(solution)/shard_map/while/body/eval_jaxpr/ppermute | solution.py:10
  324.4 4.7 conditional.8
  333.9 27.5 %collective-permute-done.2 = bf16[64,4096]{1,0:T(8,128)(2,1)S(1)} collective-permute-done((bf16[64,4096]{1,0:T(8,128)(2,1)S(1)}, bf16[64,4096]{1,0:T(8,128)(2,1)S(1)}, u32[]{:S(2)}, u32[]{:S(2)}) %collective-permute-start.2) | collective-permute-done | bytes 524320 | tf_op jit(solution)/shard_map/while/body/eval_jaxpr/ppermute | solution.py:10
  363.7 4.7 conditional.8
  373.3 22.4 %collective-permute-done.2 = bf16[64,4096]{1,0:T(8,128)(2,1)S(1)} collective-permute-done((bf16[64,4096]{1,0:T(8,128)(2,1)S(1)}, bf16[64,4096]{1,0:T(8,128)(2,1)S(1)}, u32[]{:S(2)}, u32[]{:S(2)}) %collective-permute-start.2) | collective-permute-done | bytes 524320 | tf_op jit(solution)/shard_map/while/body/eval_jaxpr/ppermute | solution.py:10
  398.0 4.7 conditional.8
  407.6 20.8 %collective-permute-done.2 = bf16[64,4096]{1,0:T(8,128)(2,1)S(1)} collective-permute-done((bf16[64,4096]{1,0:T(8,128)(2,1)S(1)}, bf16[64,4096]{1,0:T(8,128)(2,1)S(1)}, u32[]{:S(2)}, u32[]{:S(2)}) %collective-permute-start.2) | collective-permute-done | bytes 524320 | tf_op jit(solution)/shard_map/while/body/eval_jaxpr/ppermute | solution.py:10
  428.4 491.8 %while.39 = (s32[]{:T(128)}, bf16[64,4096]{1,0:T(8,128)(2,1)S(1)}, bf16[64,4096]{1,0:T(8,128)(2,1)S(1)}, bf16[2,64,4096]{2,1,0:T(8,128)(2,1)}, s32[15]{0:T(128)S...) while((s32[]{:T(128)}, bf16[64,4096]{1,0:T(8,128)(2,1)S(1)}, ...), condition=%wide.region_9.10_spmd, body=%wide.region_5.9_spmd.sunk | while | flops 557154816 | bytes 38441560 | solution.py:101
  432.5 4.7 conditional.7
  440.2 3.9 collective-permute-start
  444.2 13.3 %collective-permute-done.1 = bf16[64,4096]{1,0:T(8,128)(2,1)S(1)} collective-permute-done((bf16[64,4096]{1,0:T(8,128)(2,1)S(1)}, bf16[64,4096]{1,0:T(8,128)(2,1)S(1)}, u32[]{:S(2)}, u32[]{:S(2)}) %collective-permute-start.1) | collective-permute-done | bytes 524320 | tf_op jit(solution)/shard_map/while/body/eval_jaxpr/ppermute | solution.py:10
  457.5 10.1 %collective-permute-done = bf16[64,4096]{1,0:T(8,128)(2,1)S(1)} collective-permute-done((bf16[64,4096]{1,0:T(8,128)(2,1)S(1)}, bf16[64,4096]{1,0:T(8,128)(2,1)S(1)}, u32[]{:S(2)}, u32[]{:S(2)}) %collective-permute-start) | collective-permute-done | bytes 524320 | tf_op jit(solution)/shard_map/while/body/eval_jaxpr/ppermute | solution.py:10
  471.7 4.7 conditional.7
  483.3 13.4 %collective-permute-done.1 = bf16[64,4096]{1,0:T(8,128)(2,1)S(1)} collective-permute-done((bf16[64,4096]{1,0:T(8,128)(2,1)S(1)}, bf16[64,4096]{1,0:T(8,128)(2,1)S(1)}, u32[]{:S(2)}, u32[]{:S(2)}) %collective-permute-start.1) | collective-permute-done | bytes 524320 | tf_op jit(solution)/shard_map/while/body/eval_jaxpr/ppermute | solution.py:10
  496.8 10.1 %collective-permute-done = bf16[64,4096]{1,0:T(8,128)(2,1)S(1)} collective-permute-done((bf16[64,4096]{1,0:T(8,128)(2,1)S(1)}, bf16[64,4096]{1,0:T(8,128)(2,1)S(1)}, u32[]{:S(2)}, u32[]{:S(2)}) %collective-permute-start) | collective-permute-done | bytes 524320 | tf_op jit(solution)/shard_map/while/body/eval_jaxpr/ppermute | solution.py:10
  511.0 4.7 conditional.7
  522.7 16.8 %collective-permute-done.1 = bf16[64,4096]{1,0:T(8,128)(2,1)S(1)} collective-permute-done((bf16[64,4096]{1,0:T(8,128)(2,1)S(1)}, bf16[64,4096]{1,0:T(8,128)(2,1)S(1)}, u32[]{:S(2)}, u32[]{:S(2)}) %collective-permute-start.1) | collective-permute-done | bytes 524320 | tf_op jit(solution)/shard_map/while/body/eval_jaxpr/ppermute | solution.py:10
  539.4 10.4 %collective-permute-done = bf16[64,4096]{1,0:T(8,128)(2,1)S(1)} collective-permute-done((bf16[64,4096]{1,0:T(8,128)(2,1)S(1)}, bf16[64,4096]{1,0:T(8,128)(2,1)S(1)}, u32[]{:S(2)}, u32[]{:S(2)}) %collective-permute-start) | collective-permute-done | bytes 524320 | tf_op jit(solution)/shard_map/while/body/eval_jaxpr/ppermute | solution.py:10
  554.0 4.7 conditional.7
  565.6 9.9 %collective-permute-done.1 = bf16[64,4096]{1,0:T(8,128)(2,1)S(1)} collective-permute-done((bf16[64,4096]{1,0:T(8,128)(2,1)S(1)}, bf16[64,4096]{1,0:T(8,128)(2,1)S(1)}, u32[]{:S(2)}, u32[]{:S(2)}) %collective-permute-start.1) | collective-permute-done | bytes 524320 | tf_op jit(solution)/shard_map/while/body/eval_jaxpr/ppermute | solution.py:10
  575.5 9.3 %collective-permute-done = bf16[64,4096]{1,0:T(8,128)(2,1)S(1)} collective-permute-done((bf16[64,4096]{1,0:T(8,128)(2,1)S(1)}, bf16[64,4096]{1,0:T(8,128)(2,1)S(1)}, u32[]{:S(2)}, u32[]{:S(2)}) %collective-permute-start) | collective-permute-done | bytes 524320 | tf_op jit(solution)/shard_map/while/body/eval_jaxpr/ppermute | solution.py:10
  588.9 4.7 conditional.7
  600.5 19.0 %collective-permute-done.1 = bf16[64,4096]{1,0:T(8,128)(2,1)S(1)} collective-permute-done((bf16[64,4096]{1,0:T(8,128)(2,1)S(1)}, bf16[64,4096]{1,0:T(8,128)(2,1)S(1)}, u32[]{:S(2)}, u32[]{:S(2)}) %collective-permute-start.1) | collective-permute-done | bytes 524320 | tf_op jit(solution)/shard_map/while/body/eval_jaxpr/ppermute | solution.py:10
  619.5 10.1 %collective-permute-done = bf16[64,4096]{1,0:T(8,128)(2,1)S(1)} collective-permute-done((bf16[64,4096]{1,0:T(8,128)(2,1)S(1)}, bf16[64,4096]{1,0:T(8,128)(2,1)S(1)}, u32[]{:S(2)}, u32[]{:S(2)}) %collective-permute-start) | collective-permute-done | bytes 524320 | tf_op jit(solution)/shard_map/while/body/eval_jaxpr/ppermute | solution.py:10
  633.7 4.7 conditional.7
  641.4 3.9 collective-permute-start
  645.3 9.9 %collective-permute-done.1 = bf16[64,4096]{1,0:T(8,128)(2,1)S(1)} collective-permute-done((bf16[64,4096]{1,0:T(8,128)(2,1)S(1)}, bf16[64,4096]{1,0:T(8,128)(2,1)S(1)}, u32[]{:S(2)}, u32[]{:S(2)}) %collective-permute-start.1) | collective-permute-done | bytes 524320 | tf_op jit(solution)/shard_map/while/body/eval_jaxpr/ppermute | solution.py:10
  655.3 10.4 %collective-permute-done = bf16[64,4096]{1,0:T(8,128)(2,1)S(1)} collective-permute-done((bf16[64,4096]{1,0:T(8,128)(2,1)S(1)}, bf16[64,4096]{1,0:T(8,128)(2,1)S(1)}, u32[]{:S(2)}, u32[]{:S(2)}) %collective-permute-start) | collective-permute-done | bytes 524320 | tf_op jit(solution)/shard_map/while/body/eval_jaxpr/ppermute | solution.py:10
  669.8 4.7 conditional.7
  681.4 7.3 collective-permute-done.1
  688.8 7.9 collective-permute-done
  700.9 4.7 conditional.7
  708.5 3.9 collective-permute-start
  712.5 6.5 collective-permute-done.1
  718.9 7.9 collective-permute-done
  731.0 4.7 conditional.7
  742.6 5.6 collective-permute-done.1
  748.3 7.9 collective-permute-done
  760.3 4.7 conditional.7
  768.0 3.9 collective-permute-start
  772.0 5.2 collective-permute-done.1
  777.2 7.9 collective-permute-done
  789.3 4.7 conditional.7
  800.9 5.2 collective-permute-done.1
  806.1 7.9 collective-permute-done
  818.2 4.7 conditional.7
  829.8 5.2 collective-permute-done.1
  835.0 7.9 collective-permute-done
  847.1 4.7 conditional.7
  854.7 3.9 collective-permute-start
  858.7 5.2 collective-permute-done.1
  863.9 7.9 collective-permute-done
  882.9 5.2 collective-permute-done.1
  888.1 7.9 collective-permute-done
  907.1 5.2 collective-permute-done.1
  912.3 7.9 collective-permute-done
  (284 shorter events, 242.8 us)
Async XLA Ops:
  5.5 175.3 %copy-start.3 = (bf16[1,2,256,256]{3,2,1,0:T(8,128)(2,1)S(1)}, bf16[1,2,256,256]{3,2,1,0:T(8,128)(2,1)}, u32[]{:S(2)}) copy-start(bf16[1,2,256,256]{3,2,1,0:T(8,128)(2,1)} %param.18) | copy-start | bytes 786436
  5.5 175.3 %copy-start.4 = (f32[1,4096]{1,0:T(1,128)S(1)}, f32[1,4096]{1,0:T(1,128)}, u32[]{:S(2)}) copy-start(f32[1,4096]{1,0:T(1,128)} %param.21) | copy-start | bytes 49156
  5.5 175.3 %copy-start.5 = (bf16[1,2,4096]{2,1,0:T(2,128)(2,1)S(1)}, bf16[1,2,4096]{2,1,0:T(2,128)(2,1)}, u32[]{:S(2)}) copy-start(bf16[1,2,4096]{2,1,0:T(2,128)(2,1)} %param.20) | copy-start | bytes 49156
  5.5 174.1 %all-to-all-start = ((bf16[8,1,1,128,4096]{4,3,2,1,0:T(8,128)(2,1)}), bf16[8,1,1,128,4096]{4,3,2,1,0:T(8,128)(2,1)}, u32[]{:S(2)}, u32[]{:S(2)}) async-start(bf16[8,1,1,128,4096]{4,3,2,1,0:T(8,128)(2,1)} %stack.2), calls=%async_computation | async-start | bytes 16777216 | tf_op jit(solution)/shard_map/all_to_all | solution.py:44
  183.2 48.6 %collective-permute-start.2 = (bf16[64,4096]{1,0:T(8,128)(2,1)S(1)}, bf16[64,4096]{1,0:T(8,128)(2,1)S(1)}, u32[]{:S(2)}, u32[]{:S(2)}) collective-permute-start(bf16[64,4096]{1,0:T(8,128)(2,1)S(1)} %get-tuple-element.1181), channel_id=1, source_target_pairs={{0,32},{32,64},{64,96},{96,128},{128,160},{160,192},{192,224},{1,3... | collective-permute-start | bytes 1572872 | tf_op jit(solution)/shard_map/while/body/eval_jaxpr/ppermute | solution.py:10
  234.2 33.3 %collective-permute-start.2 = (bf16[64,4096]{1,0:T(8,128)(2,1)S(1)}, bf16[64,4096]{1,0:T(8,128)(2,1)S(1)}, u32[]{:S(2)}, u32[]{:S(2)}) collective-permute-start(bf16[64,4096]{1,0:T(8,128)(2,1)S(1)} %get-tuple-element.1181), channel_id=1, source_target_pairs={{0,32},{32,64},{64,96},{96,128},{128,160},{160,192},{192,224},{1,3... | collective-permute-start | bytes 1572872 | tf_op jit(solution)/shard_map/while/body/eval_jaxpr/ppermute | solution.py:10
  269.8 27.9 %collective-permute-start.2 = (bf16[64,4096]{1,0:T(8,128)(2,1)S(1)}, bf16[64,4096]{1,0:T(8,128)(2,1)S(1)}, u32[]{:S(2)}, u32[]{:S(2)}) collective-permute-start(bf16[64,4096]{1,0:T(8,128)(2,1)S(1)} %get-tuple-element.1181), channel_id=1, source_target_pairs={{0,32},{32,64},{64,96},{96,128},{128,160},{160,192},{192,224},{1,3... | collective-permute-start | bytes 1572872 | tf_op jit(solution)/shard_map/while/body/eval_jaxpr/ppermute | solution.py:10
  300.1 21.9 %collective-permute-start.2 = (bf16[64,4096]{1,0:T(8,128)(2,1)S(1)}, bf16[64,4096]{1,0:T(8,128)(2,1)S(1)}, u32[]{:S(2)}, u32[]{:S(2)}) collective-permute-start(bf16[64,4096]{1,0:T(8,128)(2,1)S(1)} %get-tuple-element.1181), channel_id=1, source_target_pairs={{0,32},{32,64},{64,96},{96,128},{128,160},{160,192},{192,224},{1,3... | collective-permute-start | bytes 1572872 | tf_op jit(solution)/shard_map/while/body/eval_jaxpr/ppermute | solution.py:10
  324.4 3.7 copy-start
  329.1 32.3 %collective-permute-start.2 = (bf16[64,4096]{1,0:T(8,128)(2,1)S(1)}, bf16[64,4096]{1,0:T(8,128)(2,1)S(1)}, u32[]{:S(2)}, u32[]{:S(2)}) collective-permute-start(bf16[64,4096]{1,0:T(8,128)(2,1)S(1)} %get-tuple-element.1181), channel_id=1, source_target_pairs={{0,32},{32,64},{64,96},{96,128},{128,160},{160,192},{192,224},{1,3... | collective-permute-start | bytes 1572872 | tf_op jit(solution)/shard_map/while/body/eval_jaxpr/ppermute | solution.py:10
  363.8 3.7 copy-start
  368.5 27.2 %collective-permute-start.2 = (bf16[64,4096]{1,0:T(8,128)(2,1)S(1)}, bf16[64,4096]{1,0:T(8,128)(2,1)S(1)}, u32[]{:S(2)}, u32[]{:S(2)}) collective-permute-start(bf16[64,4096]{1,0:T(8,128)(2,1)S(1)} %get-tuple-element.1181), channel_id=1, source_target_pairs={{0,32},{32,64},{64,96},{96,128},{128,160},{160,192},{192,224},{1,3... | collective-permute-start | bytes 1572872 | tf_op jit(solution)/shard_map/while/body/eval_jaxpr/ppermute | solution.py:10
  398.0 3.7 copy-start
  402.8 25.6 %collective-permute-start.2 = (bf16[64,4096]{1,0:T(8,128)(2,1)S(1)}, bf16[64,4096]{1,0:T(8,128)(2,1)S(1)}, u32[]{:S(2)}, u32[]{:S(2)}) collective-permute-start(bf16[64,4096]{1,0:T(8,128)(2,1)S(1)} %get-tuple-element.1181), channel_id=1, source_target_pairs={{0,32},{32,64},{64,96},{96,128},{128,160},{160,192},{192,224},{1,3... | collective-permute-start | bytes 1572872 | tf_op jit(solution)/shard_map/while/body/eval_jaxpr/ppermute | solution.py:10
  432.6 3.7 copy-start.1
  438.3 19.2 %collective-permute-start.1 = (bf16[64,4096]{1,0:T(8,128)(2,1)S(1)}, bf16[64,4096]{1,0:T(8,128)(2,1)S(1)}, u32[]{:S(2)}, u32[]{:S(2)}) collective-permute-start(bf16[64,4096]{1,0:T(8,128)(2,1)S(1)} %get-tuple-element.1015), channel_id=1, source_target_pairs={{32,0},{64,32},{96,64},{128,96},{160,128},{192,160},{224,192},{33,... | collective-permute-start | bytes 1572872 | tf_op jit(solution)/shard_map/while/body/eval_jaxpr/ppermute | solution.py:10
  440.2 27.4 %collective-permute-start = (bf16[64,4096]{1,0:T(8,128)(2,1)S(1)}, bf16[64,4096]{1,0:T(8,128)(2,1)S(1)}, u32[]{:S(2)}, u32[]{:S(2)}) collective-permute-start(bf16[64,4096]{1,0:T(8,128)(2,1)S(1)} %get-tuple-element.1180), channel_id=1, source_target_pairs={{0,32},{32,64},{64,96},{96,128},{128,160},{160,192},{192,224},{1,3... | collective-permute-start | bytes 1572872 | tf_op jit(solution)/shard_map/while/body/eval_jaxpr/ppermute | solution.py:10
  471.7 3.7 copy-start.1
  477.5 19.3 %collective-permute-start.1 = (bf16[64,4096]{1,0:T(8,128)(2,1)S(1)}, bf16[64,4096]{1,0:T(8,128)(2,1)S(1)}, u32[]{:S(2)}, u32[]{:S(2)}) collective-permute-start(bf16[64,4096]{1,0:T(8,128)(2,1)S(1)} %get-tuple-element.1015), channel_id=1, source_target_pairs={{32,0},{64,32},{96,64},{128,96},{160,128},{192,160},{224,192},{33,... | collective-permute-start | bytes 1572872 | tf_op jit(solution)/shard_map/while/body/eval_jaxpr/ppermute | solution.py:10
  479.4 27.5 %collective-permute-start = (bf16[64,4096]{1,0:T(8,128)(2,1)S(1)}, bf16[64,4096]{1,0:T(8,128)(2,1)S(1)}, u32[]{:S(2)}, u32[]{:S(2)}) collective-permute-start(bf16[64,4096]{1,0:T(8,128)(2,1)S(1)} %get-tuple-element.1180), channel_id=1, source_target_pairs={{0,32},{32,64},{64,96},{96,128},{128,160},{160,192},{192,224},{1,3... | collective-permute-start | bytes 1572872 | tf_op jit(solution)/shard_map/while/body/eval_jaxpr/ppermute | solution.py:10
  511.1 3.7 copy-start.1
  516.8 22.6 %collective-permute-start.1 = (bf16[64,4096]{1,0:T(8,128)(2,1)S(1)}, bf16[64,4096]{1,0:T(8,128)(2,1)S(1)}, u32[]{:S(2)}, u32[]{:S(2)}) collective-permute-start(bf16[64,4096]{1,0:T(8,128)(2,1)S(1)} %get-tuple-element.1015), channel_id=1, source_target_pairs={{32,0},{64,32},{96,64},{128,96},{160,128},{192,160},{224,192},{33,... | collective-permute-start | bytes 1572872 | tf_op jit(solution)/shard_map/while/body/eval_jaxpr/ppermute | solution.py:10
  518.7 31.1 %collective-permute-start = (bf16[64,4096]{1,0:T(8,128)(2,1)S(1)}, bf16[64,4096]{1,0:T(8,128)(2,1)S(1)}, u32[]{:S(2)}, u32[]{:S(2)}) collective-permute-start(bf16[64,4096]{1,0:T(8,128)(2,1)S(1)} %get-tuple-element.1180), channel_id=1, source_target_pairs={{0,32},{32,64},{64,96},{96,128},{128,160},{160,192},{192,224},{1,3... | collective-permute-start | bytes 1572872 | tf_op jit(solution)/shard_map/while/body/eval_jaxpr/ppermute | solution.py:10
  554.0 3.7 copy-start.1
  559.8 15.7 %collective-permute-start.1 = (bf16[64,4096]{1,0:T(8,128)(2,1)S(1)}, bf16[64,4096]{1,0:T(8,128)(2,1)S(1)}, u32[]{:S(2)}, u32[]{:S(2)}) collective-permute-start(bf16[64,4096]{1,0:T(8,128)(2,1)S(1)} %get-tuple-element.1015), channel_id=1, source_target_pairs={{32,0},{64,32},{96,64},{128,96},{160,128},{192,160},{224,192},{33,... | collective-permute-start | bytes 1572872 | tf_op jit(solution)/shard_map/while/body/eval_jaxpr/ppermute | solution.py:10
  561.7 23.1 %collective-permute-start = (bf16[64,4096]{1,0:T(8,128)(2,1)S(1)}, bf16[64,4096]{1,0:T(8,128)(2,1)S(1)}, u32[]{:S(2)}, u32[]{:S(2)}) collective-permute-start(bf16[64,4096]{1,0:T(8,128)(2,1)S(1)} %get-tuple-element.1180), channel_id=1, source_target_pairs={{0,32},{32,64},{64,96},{96,128},{128,160},{160,192},{192,224},{1,3... | collective-permute-start | bytes 1572872 | tf_op jit(solution)/shard_map/while/body/eval_jaxpr/ppermute | solution.py:10
  588.9 3.7 copy-start.1
  594.7 24.8 %collective-permute-start.1 = (bf16[64,4096]{1,0:T(8,128)(2,1)S(1)}, bf16[64,4096]{1,0:T(8,128)(2,1)S(1)}, u32[]{:S(2)}, u32[]{:S(2)}) collective-permute-start(bf16[64,4096]{1,0:T(8,128)(2,1)S(1)} %get-tuple-element.1015), channel_id=1, source_target_pairs={{32,0},{64,32},{96,64},{128,96},{160,128},{192,160},{224,192},{33,... | collective-permute-start | bytes 1572872 | tf_op jit(solution)/shard_map/while/body/eval_jaxpr/ppermute | solution.py:10
  596.6 33.0 %collective-permute-start = (bf16[64,4096]{1,0:T(8,128)(2,1)S(1)}, bf16[64,4096]{1,0:T(8,128)(2,1)S(1)}, u32[]{:S(2)}, u32[]{:S(2)}) collective-permute-start(bf16[64,4096]{1,0:T(8,128)(2,1)S(1)} %get-tuple-element.1180), channel_id=1, source_target_pairs={{0,32},{32,64},{64,96},{96,128},{128,160},{160,192},{192,224},{1,3... | collective-permute-start | bytes 1572872 | tf_op jit(solution)/shard_map/while/body/eval_jaxpr/ppermute | solution.py:10
  633.7 3.7 copy-start.1
  639.5 15.8 %collective-permute-start.1 = (bf16[64,4096]{1,0:T(8,128)(2,1)S(1)}, bf16[64,4096]{1,0:T(8,128)(2,1)S(1)}, u32[]{:S(2)}, u32[]{:S(2)}) collective-permute-start(bf16[64,4096]{1,0:T(8,128)(2,1)S(1)} %get-tuple-element.1015), channel_id=1, source_target_pairs={{32,0},{64,32},{96,64},{128,96},{160,128},{192,160},{224,192},{33,... | collective-permute-start | bytes 1572872 | tf_op jit(solution)/shard_map/while/body/eval_jaxpr/ppermute | solution.py:10
  641.4 24.3 %collective-permute-start = (bf16[64,4096]{1,0:T(8,128)(2,1)S(1)}, bf16[64,4096]{1,0:T(8,128)(2,1)S(1)}, u32[]{:S(2)}, u32[]{:S(2)}) collective-permute-start(bf16[64,4096]{1,0:T(8,128)(2,1)S(1)} %get-tuple-element.1180), channel_id=1, source_target_pairs={{0,32},{32,64},{64,96},{96,128},{128,160},{160,192},{192,224},{1,3... | collective-permute-start | bytes 1572872 | tf_op jit(solution)/shard_map/while/body/eval_jaxpr/ppermute | solution.py:10
  669.8 3.7 copy-start.1
  675.6 13.2 %collective-permute-start.1 = (bf16[64,4096]{1,0:T(8,128)(2,1)S(1)}, bf16[64,4096]{1,0:T(8,128)(2,1)S(1)}, u32[]{:S(2)}, u32[]{:S(2)}) collective-permute-start(bf16[64,4096]{1,0:T(8,128)(2,1)S(1)} %get-tuple-element.1015), channel_id=1, source_target_pairs={{32,0},{64,32},{96,64},{128,96},{160,128},{192,160},{224,192},{33,... | collective-permute-start | bytes 1572872 | tf_op jit(solution)/shard_map/while/body/eval_jaxpr/ppermute | solution.py:10
  677.5 19.2 %collective-permute-start = (bf16[64,4096]{1,0:T(8,128)(2,1)S(1)}, bf16[64,4096]{1,0:T(8,128)(2,1)S(1)}, u32[]{:S(2)}, u32[]{:S(2)}) collective-permute-start(bf16[64,4096]{1,0:T(8,128)(2,1)S(1)} %get-tuple-element.1180), channel_id=1, source_target_pairs={{0,32},{32,64},{64,96},{96,128},{128,160},{160,192},{192,224},{1,3... | collective-permute-start | bytes 1572872 | tf_op jit(solution)/shard_map/while/body/eval_jaxpr/ppermute | solution.py:10
  700.9 3.7 copy-start.1
  706.6 12.3 %collective-permute-start.1 = (bf16[64,4096]{1,0:T(8,128)(2,1)S(1)}, bf16[64,4096]{1,0:T(8,128)(2,1)S(1)}, u32[]{:S(2)}, u32[]{:S(2)}) collective-permute-start(bf16[64,4096]{1,0:T(8,128)(2,1)S(1)} %get-tuple-element.1015), channel_id=1, source_target_pairs={{32,0},{64,32},{96,64},{128,96},{160,128},{192,160},{224,192},{33,... | collective-permute-start | bytes 1572872 | tf_op jit(solution)/shard_map/while/body/eval_jaxpr/ppermute | solution.py:10
  708.5 18.4 %collective-permute-start = (bf16[64,4096]{1,0:T(8,128)(2,1)S(1)}, bf16[64,4096]{1,0:T(8,128)(2,1)S(1)}, u32[]{:S(2)}, u32[]{:S(2)}) collective-permute-start(bf16[64,4096]{1,0:T(8,128)(2,1)S(1)} %get-tuple-element.1180), channel_id=1, source_target_pairs={{0,32},{32,64},{64,96},{96,128},{128,160},{160,192},{192,224},{1,3... | collective-permute-start | bytes 1572872 | tf_op jit(solution)/shard_map/while/body/eval_jaxpr/ppermute | solution.py:10
  731.0 3.7 copy-start.1
  736.8 11.5 %collective-permute-start.1 = (bf16[64,4096]{1,0:T(8,128)(2,1)S(1)}, bf16[64,4096]{1,0:T(8,128)(2,1)S(1)}, u32[]{:S(2)}, u32[]{:S(2)}) collective-permute-start(bf16[64,4096]{1,0:T(8,128)(2,1)S(1)} %get-tuple-element.1015), channel_id=1, source_target_pairs={{32,0},{64,32},{96,64},{128,96},{160,128},{192,160},{224,192},{33,... | collective-permute-start | bytes 1572872 | tf_op jit(solution)/shard_map/while/body/eval_jaxpr/ppermute | solution.py:10
  738.7 17.5 %collective-permute-start = (bf16[64,4096]{1,0:T(8,128)(2,1)S(1)}, bf16[64,4096]{1,0:T(8,128)(2,1)S(1)}, u32[]{:S(2)}, u32[]{:S(2)}) collective-permute-start(bf16[64,4096]{1,0:T(8,128)(2,1)S(1)} %get-tuple-element.1180), channel_id=1, source_target_pairs={{0,32},{32,64},{64,96},{96,128},{128,160},{160,192},{192,224},{1,3... | collective-permute-start | bytes 1572872 | tf_op jit(solution)/shard_map/while/body/eval_jaxpr/ppermute | solution.py:10
  760.4 3.7 copy-start.1
  766.1 11.1 %collective-permute-start.1 = (bf16[64,4096]{1,0:T(8,128)(2,1)S(1)}, bf16[64,4096]{1,0:T(8,128)(2,1)S(1)}, u32[]{:S(2)}, u32[]{:S(2)}) collective-permute-start(bf16[64,4096]{1,0:T(8,128)(2,1)S(1)} %get-tuple-element.1015), channel_id=1, source_target_pairs={{32,0},{64,32},{96,64},{128,96},{160,128},{192,160},{224,192},{33,... | collective-permute-start | bytes 1572872 | tf_op jit(solution)/shard_map/while/body/eval_jaxpr/ppermute | solution.py:10
  768.0 17.1 %collective-permute-start = (bf16[64,4096]{1,0:T(8,128)(2,1)S(1)}, bf16[64,4096]{1,0:T(8,128)(2,1)S(1)}, u32[]{:S(2)}, u32[]{:S(2)}) collective-permute-start(bf16[64,4096]{1,0:T(8,128)(2,1)S(1)} %get-tuple-element.1180), channel_id=1, source_target_pairs={{0,32},{32,64},{64,96},{96,128},{128,160},{160,192},{192,224},{1,3... | collective-permute-start | bytes 1572872 | tf_op jit(solution)/shard_map/while/body/eval_jaxpr/ppermute | solution.py:10
  789.3 3.7 copy-start.1
  795.0 11.1 %collective-permute-start.1 = (bf16[64,4096]{1,0:T(8,128)(2,1)S(1)}, bf16[64,4096]{1,0:T(8,128)(2,1)S(1)}, u32[]{:S(2)}, u32[]{:S(2)}) collective-permute-start(bf16[64,4096]{1,0:T(8,128)(2,1)S(1)} %get-tuple-element.1015), channel_id=1, source_target_pairs={{32,0},{64,32},{96,64},{128,96},{160,128},{192,160},{224,192},{33,... | collective-permute-start | bytes 1572872 | tf_op jit(solution)/shard_map/while/body/eval_jaxpr/ppermute | solution.py:10
  796.9 17.1 %collective-permute-start = (bf16[64,4096]{1,0:T(8,128)(2,1)S(1)}, bf16[64,4096]{1,0:T(8,128)(2,1)S(1)}, u32[]{:S(2)}, u32[]{:S(2)}) collective-permute-start(bf16[64,4096]{1,0:T(8,128)(2,1)S(1)} %get-tuple-element.1180), channel_id=1, source_target_pairs={{0,32},{32,64},{64,96},{96,128},{128,160},{160,192},{192,224},{1,3... | collective-permute-start | bytes 1572872 | tf_op jit(solution)/shard_map/while/body/eval_jaxpr/ppermute | solution.py:10
  818.2 3.7 copy-start.1
  823.9 11.1 %collective-permute-start.1 = (bf16[64,4096]{1,0:T(8,128)(2,1)S(1)}, bf16[64,4096]{1,0:T(8,128)(2,1)S(1)}, u32[]{:S(2)}, u32[]{:S(2)}) collective-permute-start(bf16[64,4096]{1,0:T(8,128)(2,1)S(1)} %get-tuple-element.1015), channel_id=1, source_target_pairs={{32,0},{64,32},{96,64},{128,96},{160,128},{192,160},{224,192},{33,... | collective-permute-start | bytes 1572872 | tf_op jit(solution)/shard_map/while/body/eval_jaxpr/ppermute | solution.py:10
  825.8 17.1 %collective-permute-start = (bf16[64,4096]{1,0:T(8,128)(2,1)S(1)}, bf16[64,4096]{1,0:T(8,128)(2,1)S(1)}, u32[]{:S(2)}, u32[]{:S(2)}) collective-permute-start(bf16[64,4096]{1,0:T(8,128)(2,1)S(1)} %get-tuple-element.1180), channel_id=1, source_target_pairs={{0,32},{32,64},{64,96},{96,128},{128,160},{160,192},{192,224},{1,3... | collective-permute-start | bytes 1572872 | tf_op jit(solution)/shard_map/while/body/eval_jaxpr/ppermute | solution.py:10
  847.1 3.7 copy-start.1
  852.8 11.1 %collective-permute-start.1 = (bf16[64,4096]{1,0:T(8,128)(2,1)S(1)}, bf16[64,4096]{1,0:T(8,128)(2,1)S(1)}, u32[]{:S(2)}, u32[]{:S(2)}) collective-permute-start(bf16[64,4096]{1,0:T(8,128)(2,1)S(1)} %get-tuple-element.1015), channel_id=1, source_target_pairs={{32,0},{64,32},{96,64},{128,96},{160,128},{192,160},{224,192},{33,... | collective-permute-start | bytes 1572872 | tf_op jit(solution)/shard_map/while/body/eval_jaxpr/ppermute | solution.py:10
  854.7 17.1 %collective-permute-start = (bf16[64,4096]{1,0:T(8,128)(2,1)S(1)}, bf16[64,4096]{1,0:T(8,128)(2,1)S(1)}, u32[]{:S(2)}, u32[]{:S(2)}) collective-permute-start(bf16[64,4096]{1,0:T(8,128)(2,1)S(1)} %get-tuple-element.1180), channel_id=1, source_target_pairs={{0,32},{32,64},{64,96},{96,128},{128,160},{160,192},{192,224},{1,3... | collective-permute-start | bytes 1572872 | tf_op jit(solution)/shard_map/while/body/eval_jaxpr/ppermute | solution.py:10
  877.0 11.1 %collective-permute-start.1 = (bf16[64,4096]{1,0:T(8,128)(2,1)S(1)}, bf16[64,4096]{1,0:T(8,128)(2,1)S(1)}, u32[]{:S(2)}, u32[]{:S(2)}) collective-permute-start(bf16[64,4096]{1,0:T(8,128)(2,1)S(1)} %get-tuple-element.1015), channel_id=1, source_target_pairs={{32,0},{64,32},{96,64},{128,96},{160,128},{192,160},{224,192},{33,... | collective-permute-start | bytes 1572872 | tf_op jit(solution)/shard_map/while/body/eval_jaxpr/ppermute | solution.py:10
  878.9 17.1 %collective-permute-start = (bf16[64,4096]{1,0:T(8,128)(2,1)S(1)}, bf16[64,4096]{1,0:T(8,128)(2,1)S(1)}, u32[]{:S(2)}, u32[]{:S(2)}) collective-permute-start(bf16[64,4096]{1,0:T(8,128)(2,1)S(1)} %get-tuple-element.1180), channel_id=1, source_target_pairs={{0,32},{32,64},{64,96},{96,128},{128,160},{160,192},{192,224},{1,3... | collective-permute-start | bytes 1572872 | tf_op jit(solution)/shard_map/while/body/eval_jaxpr/ppermute | solution.py:10
  901.2 11.1 %collective-permute-start.1 = (bf16[64,4096]{1,0:T(8,128)(2,1)S(1)}, bf16[64,4096]{1,0:T(8,128)(2,1)S(1)}, u32[]{:S(2)}, u32[]{:S(2)}) collective-permute-start(bf16[64,4096]{1,0:T(8,128)(2,1)S(1)} %get-tuple-element.1015), channel_id=1, source_target_pairs={{32,0},{64,32},{96,64},{128,96},{160,128},{192,160},{224,192},{33,... | collective-permute-start | bytes 1572872 | tf_op jit(solution)/shard_map/while/body/eval_jaxpr/ppermute | solution.py:10
  903.1 17.1 %collective-permute-start = (bf16[64,4096]{1,0:T(8,128)(2,1)S(1)}, bf16[64,4096]{1,0:T(8,128)(2,1)S(1)}, u32[]{:S(2)}, u32[]{:S(2)}) collective-permute-start(bf16[64,4096]{1,0:T(8,128)(2,1)S(1)} %get-tuple-element.1180), channel_id=1, source_target_pairs={{0,32},{32,64},{64,96},{96,128},{128,160},{160,192},{192,224},{1,3... | collective-permute-start | bytes 1572872 | tf_op jit(solution)/shard_map/while/body/eval_jaxpr/ppermute | solution.py:10
